TPU v7x, 32 devices: a whole 2x2x4 slice. The times are simulated.
32 devices in a mesh: section: 2 (over x), ex: 4 (over z), ey: 4 (over y, core).
Axes of the slice: x: 2, y: 2, z: 4, core: 2. Of those that a mesh axis runs over, the one named last changes fastest.
Arguments:
- section_out: bfloat16 [2, 1024, 7168], P('section', ('ex', 'ey')), may hold values from -6 to 6
- expert_ids: int32 [2, 1024, 2], P('section', ('ex', 'ey')), may hold values from 0 to 3, all different within a row; in each aligned block of 64 rows (0 to 63, 64 to 127, ..., all dimensions but the last counted through in order) at most 48 rows name the same one
- gate_weights: float32 [2, 1024, 2], P('section', ('ex', 'ey')), may hold values from 0.1 to 1
- w_gate_up: bfloat16 [2, 4, 7168, 2, 1024], P('section', 'ey', None, None, 'ex'), may hold values from -0.0625 to 0.0625
- w_down: bfloat16 [2, 4, 1024, 7168], P('section', 'ey', 'ex'), may hold values from -0.1875 to 0.1875
Outputs:
- next_state: bfloat16 [2, 1024, 7168], P('section', ('ex', 'ey'))
Inputs may be any that keep to these rules, and one draw needn't show every extreme that they name: `expert_ids`: each row names 2 different experts. In the rows of one device (aligned blocks of 64 rows, all leading dimensions in order) no expert is named by more than 48 rows, and some block of every draw names one expert exactly 48 times.
All inputs are finite; a program needn't handle non-finite values.
Results may differ from a plain program's by a relative error of at most 0.008.
Values may be sent and summed in bfloat16 or wider, within the bound.
A program may use at most 128 MiB of HBM per device.

v0:
```python
import jax
import jax.numpy as jnp
from jax import lax
from jax.sharding import PartitionSpec as P


def shifted(value, axis, steps):
    count = lax.axis_size(axis)
    pairs = [(source, (source + steps) % count) for source in range(count)]
    return lax.ppermute(value, axis, pairs)


def expert_hidden(token_rows, gate_up, unit_count):
    mixed = jnp.dot(token_rows, gate_up, preferred_element_type=jnp.float32)
    return (jax.nn.silu(mixed[:, :unit_count]) * mixed[:, unit_count:]).astype(jnp.bfloat16)


def on_device(section_out, expert_ids, gate_weights, w_gate_up, w_down):
    tok_rows = section_out.shape[1]
    model_width = section_out.shape[2]
    top_count = expert_ids.shape[2]
    experts = lax.axis_size("ey")
    capacity = min(tok_rows, 3 * tok_rows * top_count // (2 * experts))
    unit_count = w_down.shape[2]
    gate_up = w_gate_up[0, 0].reshape(model_width, 2 * unit_count)
    down_rows = w_down[0, 0]
    incoming = shifted(section_out, "section", 1)[0]
    chosen = expert_ids[0].reshape(-1)
    one_hot = (chosen[:, None] == jnp.arange(experts, dtype=jnp.int32)[None, :]).astype(jnp.int32)
    slot_rank = jnp.sum((jnp.cumsum(one_hot, axis=0) - one_hot) * one_hot, axis=1)
    position = chosen * capacity + slot_rank
    token_of = jnp.arange(tok_rows * top_count, dtype=jnp.int32) // top_count
    filled = jnp.zeros((experts * capacity,), jnp.int32).at[position].set(1)
    source_row = jnp.zeros((experts * capacity,), jnp.int32).at[position].set(token_of)
    outgoing = jnp.where(filled[:, None] > 0, incoming[source_row], jnp.zeros((), jnp.bfloat16))
    arrived = lax.all_to_all(
        outgoing.reshape(experts, capacity, model_width),
        "ey",
        split_axis=0,
        concat_axis=0,
        tiled=True,
    ).reshape(experts * capacity, model_width)
    hidden_all = expert_hidden(
        lax.all_gather(arrived, "ex", axis=0, tiled=True), gate_up, unit_count
    )
    summed = lax.psum_scatter(
        jnp.dot(hidden_all, down_rows, preferred_element_type=jnp.float32).astype(jnp.bfloat16),
        "ex",
        scatter_dimension=0,
        tiled=True,
    )
    expert_out = lax.all_to_all(
        summed.reshape(experts, capacity, model_width),
        "ey",
        split_axis=0,
        concat_axis=0,
        tiled=True,
    ).reshape(experts * capacity, model_width)
    picked = expert_out[position].reshape(tok_rows, top_count, model_width)
    weighted = jnp.einsum("tkd,tk->td", picked.astype(jnp.float32), gate_weights[0])
    result = (incoming.astype(jnp.float32) + weighted).astype(jnp.bfloat16)
    return result[None]


def solution(mesh):
    return jax.shard_map(
        on_device,
        mesh=mesh,
        in_specs=(
            P("section", ("ex", "ey"), None),
            P("section", ("ex", "ey"), None),
            P("section", ("ex", "ey"), None),
            P("section", "ey", None, None, "ex"),
            P("section", "ey", "ex", None),
        ),
        out_specs=P("section", ("ex", "ey"), None),
        check_vma=False,
    )
```

profile of v0, /device:TPU:0, one launch (start us, length us, event | category | flops | bytes accessed | tf_op | source)
XLA Modules:
  0.0 523.0 jit_solution(17664300272078709261)
XLA Ops:
  6.5 0.0 all-gather.2.cloned.1.call-start
  6.5 3.0 collective-permute-start
  9.5 0.8 copy.9
  10.3 0.7 broadcast_multiply_fusion
  11.0 0.1 eq.15
  11.1 0.1 fusion.6
  11.2 0.1 copy.8
  11.3 0.1 mul.28
  11.4 0.2 reduce_window_sum.11
  11.6 0.2 select_reduce_fusion
  11.8 1.0 scatter_custom_fusion.1
  12.8 1.0 scatter_custom_fusion
  13.8 0.1 broadcast_in_dim.29
  13.9 16.2 %collective-permute-done = bf16[1,64,7168]{2,1,0:T(8,128)(2,1)S(1)} collective-permute-done((bf16[1,64,7168]{2,1,0:T(8,128)(2,1)}, bf16[1,64,7168]{2,1,0:T(8,128)(2,1)S(1)}, u32[]{:S(2)}, u32[]{:S(2)}) %collective-permute-start) | collective-permute-done | bytes 917536 | tf_op jit(solution)/shard_map/ppermute | solution.py:10
  30.1 3.8 gather_fusion
  33.9 2.0 broadcast_select_fusion
  35.9 36.0 %all_to_all.10 = bf16[4,48,7168]{2,1,0:T(8,128)(2,1)} all-to-all(bf16[4,48,7168]{2,1,0:T(8,128)(2,1)S(1)} %broadcast_select_fusion), channel_id=1, replica_groups=mesh['section'=2,'ex'=4,'ey'=4] {'ey'}, dimensions={0} | all-to-all | bytes 5505024 | tf_op jit(solution)/shard_map/all_to_all | solution.py:36
  71.9 0.0 all-gather.2.cloned.1.call-update
  72.0 0.0 reduce-scatter.2.cloned.1.call-start
  72.0 7.4 %copy.12 = bf16[896,8,2,256]{3,1,2,0:T(8,128)(2,1)} copy(bf16[896,8,2,256]{3,2,1,0:T(2,128)(2,1)} %bitcast.35) | data formatting | bytes 14680064
  79.4 185.8 %all-gather.2.cloned.1.call-done = bf16[768,7168]{1,0:T(8,128)(2,1)} async-done(((bf16[192,7168]{1,0:T(8,128)(2,1)}), bf16[768,7168]{1,0:T(8,128)(2,1)}) %all-gather.2.cloned.1.call-update) | async-done | bytes 11010064 | tf_op jit(solution)/shard_map/all_gather | solution.py:44
  265.1 10.9 %fusion.13 = f32[768,512]{1,0:T(8,128)S(1)} fusion(bf16[768,7168]{1,0:T(8,128)(2,1)} %all-gather.2.cloned.1.call-done, bf16[7168,512]{1,0:T(8,128)(2,1)} %bitcast.36), kind=kOutput, calls=%fused_computation.33 | convolution fusion | flops 5637144576 | bytes 19922944 | tf_op jit(solution)/shard_map/dot_general | solution.py:14
  276.0 5.8 %convolution_convert_fusion = bf16[768,7168]{1,0:T(8,128)(2,1)} fusion(bf16[1,1,256,7168]{3,2,1,0:T(8,128)(2,1)S(1)} %copy-done, f32[768,512]{1,0:T(8,128)S(1)} %fusion.13), kind=kOutput, calls=%fused_computation.4 | convolution fusion | flops 2825256960 | bytes 16252928 | tf_op jit(solution)/shard_map/dot_general | solution.py:47
  281.8 0.0 reduce-scatter.2.cloned.1.call-update
  281.8 184.8 %reduce-scatter.2.cloned.1.call-done = bf16[192,7168]{1,0:T(8,128)(2,1)} async-done(((bf16[768,7168]{1,0:T(8,128)(2,1)}), bf16[192,7168]{1,0:T(8,128)(2,1)}) %reduce-scatter.2.cloned.1.call-update) | async-done | bytes 2752528 | tf_op jit(solution)/shard_map/reduce_scatter | solution.py:46
  466.7 4.9 all-to-all-start.1
  471.6 0.1 copy.10
  471.7 32.4 %all-to-all-done.1 = bf16[4,48,7168]{2,1,0:T(8,128)(2,1)} async-done(((bf16[4,48,7168]{2,1,0:T(8,128)(2,1)}), bf16[4,48,7168]{2,1,0:T(8,128)(2,1)}, u32[]{:S(2)}, u32[]{:S(2)}) %all-to-all-start.1) | async-done | bytes 2752544 | tf_op jit(solution)/shard_map/all_to_all | solution.py:52
  504.1 5.5 %gather_fusion.1 = bf16[128,7168]{1,0:T(8,128)(2,1)S(1)} fusion(bf16[192,7168]{1,0:T(8,128)(2,1)} %bitcast.7, s32[1024]{0:T(1024)S(1)} %pad_clamp_fusion), kind=kCustom, calls=%fused_computation.1 | custom fusion | bytes 3670528 | tf_op jit(solution)/shard_map/gather | solution.py:59
  509.6 1.7 reshape.53
  511.3 3.5 fusion.14
  514.9 1.3 fusion.2
  (11 shorter events, 0.0 us)
Async XLA Ops:
  6.5 258.6 %all-gather.2.cloned.1.call-start = ((), (), s32[]{:S(2)}) async-start(), calls=%async_computation.3 | async-start | bytes 13762560 | tf_op jit(solution)/shard_map/all_gather | solution.py:44
  6.5 23.5 %collective-permute-start = (bf16[1,64,7168]{2,1,0:T(8,128)(2,1)}, bf16[1,64,7168]{2,1,0:T(8,128)(2,1)S(1)}, u32[]{:S(2)}, u32[]{:S(2)}) collective-permute-start(bf16[1,64,7168]{2,1,0:T(8,128)(2,1)} %param.5), channel_id=1, source_target_pairs={{0,16},{16,0},{1,17},{17,1},{2,18},{18,2},{3,19},{19,3},{4,20},{20... | collective-permute-start | bytes 2752520 | tf_op jit(solution)/shard_map/ppermute | solution.py:10
  72.0 394.7 %reduce-scatter.2.cloned.1.call-start = ((), (), s32[]{:S(2)}) async-start(), calls=%async_computation.4 | async-start | bytes 13762560 | tf_op jit(solution)/shard_map/reduce_scatter | solution.py:46
  265.1 10.9 %copy-start = (bf16[1,1,256,7168]{3,2,1,0:T(8,128)(2,1)S(1)}, bf16[1,1,256,7168]{3,2,1,0:T(8,128)(2,1)}, u32[]{:S(2)}) copy-start(bf16[1,1,256,7168]{3,2,1,0:T(8,128)(2,1)} %param.9) | copy-start | bytes 11010052
  466.6 4.9 copy-start.1
  466.7 37.5 %all-to-all-start.1 = ((bf16[4,48,7168]{2,1,0:T(8,128)(2,1)}), bf16[4,48,7168]{2,1,0:T(8,128)(2,1)}, u32[]{:S(2)}, u32[]{:S(2)}) async-start(bf16[4,48,7168]{2,1,0:T(8,128)(2,1)} %bitcast.37), calls=%async_computation.2 | async-start | bytes 5505024 | tf_op jit(solution)/shard_map/all_to_all | solution.py:52
Sparse Core Ops, SparseCore 0:
  72.1 193.0 all-gather.1
  281.9 184.6 reduce-scatter.1
where the time goes:
time: 523 us
  waiting for transfers between devices  419 us (80%)
  blocking collectives  36 us (7%)
  local copies, waits for them, and re-layouts  21.7 us (4%)
  matrix products  20.2 us (4%)
  between operations  13.5 us (3%)
  starting transfers between devices  7.89 us (2%)
    all_gather x1, waiting for transfers between devices, on_device(): lax.all_gather(arrived, 'ex', axis=0, tiled=True)  186 us
    reduce_scatter x1, waiting for transfers between devices, on_device(): lax.psum_scatter(jnp.dot(hidden_all, down_rows, preferred_element_type=jn...  185 us
    all_to_all x1, blocking collectives, on_device(): lax.all_to_all(outgoing.reshape(experts, capacity, model_width), 'ey', sp...  36 us
    all_to_all x1, waiting for transfers between devices, on_device(): lax.all_to_all(summed.reshape(experts, capacity, model_width), 'ey', spli...  32.4 us
    ppermute x1, waiting for transfers between devices, shifted(): return lax.ppermute(value, axis, pairs)  16.2 us
    dot_general x1, matrix products, expert_hidden(): mixed = jnp.dot(token_rows, gate_up, preferred_element_type=jnp.float32)  10.9 us
  transfers between devices with their start and end apart: 4, of which 4 were waited for; matrix products, arithmetic and copies ran while one was open for 2% of the time, Pallas kernels for 0%

commit v1 on v0

v1 whole, which is shorter than its diff:
```python
import functools
import jax
import jax.numpy as jnp
from jax import lax
from jax.experimental import pallas as pl
from jax.experimental.pallas import tpu as pltpu
from jax.sharding import PartitionSpec as P

LANES = 128
VMEM_BYTES = 67043328
MESH = pl.DeviceIdType.MESH
F32, BF16 = jnp.float32, jnp.bfloat16


def spans_of(width, parts):
    tiles = width // LANES
    first = max(1, tiles * 10 // 56)
    cuts = [0, first * LANES]
    for i in range(parts - 1):
        cuts.append((first + (tiles - first) * (i + 1) // (parts - 1)) * LANES)
    return tuple((a, b - a) for a, b in zip(cuts[:-1], cuts[1:]))


def even_spans(width, parts):
    tiles = width // LANES
    cuts = [tiles * i // parts * LANES for i in range(parts + 1)]
    return tuple((a, b - a) for a, b in zip(cuts[:-1], cuts[1:]))


def fused_kernel(S, E, EY, R, D, U, CAPW, ag_spans, y_first, rs_spans, ktile, ntile,
                 x_ref, cw_ref, wgu_ref, wd_ref, out_ref,
                 tok, part, wgu, wd, hid, mix, acc, cw_all, sib_in, y_in, z_in,
                 w_sem, shift_s, ag_r, zs, ys, ss, cw_s, cw_r,
                 rsib_s, rsib_r, ry_s, ry_r, rz_s, rz_r):
    Y = EY // 2
    s, e, yc = lax.axis_index("section"), lax.axis_index("ex"), lax.axis_index("ey")
    y, c = yc // 2, yc % 2
    sib = {"ey": 2 * y + (1 - c)}

    barrier = pltpu.get_barrier_semaphore()
    others = [(i, j) for i in range(E) for j in range(EY) if i or j]
    for i, j in others:
        pl.semaphore_signal(barrier, inc=1, device_id={"ex": (e + i) % E, "ey": (yc + j) % EY}, device_id_type=MESH)
    for d in (1, S - 1):
        pl.semaphore_signal(barrier, inc=1, device_id={"section": (s + d) % S}, device_id_type=MESH)
    loads = [pltpu.make_async_copy(wgu_ref, wgu, w_sem.at[0]), pltpu.make_async_copy(wd_ref, wd, w_sem.at[1])]
    for load in loads:
        load.start()
    pl.semaphore_wait(barrier, len(others) + 2)

    def remote(src, dst, send, recv, device):
        return pltpu.make_async_remote_copy(src_ref=src, dst_ref=dst, send_sem=send, recv_sem=recv,
                                            device_id=device, device_id_type=MESH)

    def rows(core):
        return pl.ds(pl.multiple_of(core * R, R), R)

    def block(ee, cc, h):
        return tok.at[ee, rows(cc), pl.ds(*ag_spans[h])]

    def shift_copy(h):
        return remote(x_ref.at[:, pl.ds(*ag_spans[h])], block(e, yc, h), shift_s.at[h], ag_r.at[e, yc, h],
                      {"section": (s + 1) % S})

    def z_copy(way, ee, yy, h):
        step = 1 - 2 * way
        b = block(ee, 2 * yy + c, h)
        return remote(b, b, zs.at[way, ee, yy, h], ag_r.at[ee, 2 * yy + c, h], {"ex": e + step})

    def y_copy(i, ee, h):
        b = block(ee, yc, h)
        return remote(b, b, ys.at[i, ee, h], ag_r.at[ee, yc, h], {"ey": (yc + 2 * (i + 1)) % EY})

    def sib_copy(ee, yy, h):
        b = block(ee, 2 * yy + c, h)
        return remote(b, b, ss.at[ee, yy, h], ag_r.at[ee, 2 * yy + c, h], sib)

    def arrived(ee, cc, h):
        b = block(ee, cc, h)
        remote(b, b, ss.at[0, 0, 0], ag_r.at[ee, cc, h], sib).wait_recv()

    for h in range(len(ag_spans)):
        shift_copy(h).start()

    def cw_copy(i, j):
        return remote(cw_ref, cw_all.at[e, yc], cw_s.at[i, j], cw_r.at[e, yc],
                      {"ex": (e + i) % E, "ey": (yc + j) % EY})

    for i, j in others:
        cw_copy(i, j).start()
    cw_all[e, yc] = cw_ref[...]

    def spread(ee, yy, h, k, side):
        sib_copy(ee, yy, h).start()
        if side in (None, 0):
            @pl.when(e < E - 1)
            def _():
                z_copy(0, ee, yy, h).start()
        if side in (None, 1):
            @pl.when(e > 0)
            def _():
                z_copy(1, ee, yy, h).start()

    def side_blocks(k):
        if k == 0:
            return [(None, e, None)]
        return [(0, e - k, e >= k), (1, e + k, e + k < E)]

    def guarded(cond, fn):
        if cond is None:
            fn()
        else:
            pl.when(cond)(fn)

    def others_of(y0):
        return [(y0 + 1 + i) % Y for i in range(Y - 1)]

    def z_stage(k):
        for h in range(len(ag_spans)):
            for side, ee, cond in side_blocks(k):
                def go(side=side, ee=ee, h=h):
                    first = h < y_first
                    arrived(ee, yc, h)
                    if not first or k == 0:
                        for i in range(Y - 1):
                            y_copy(i, ee, h).start()
                    spread(ee, y, h, k, side)
                    if first and k > 0:
                        for yy in others_of(y):
                            arrived(ee, 2 * yy + c, h)
                            spread(ee, yy, h, k, side)
                guarded(cond, go)
        if k == 0:
            for h in range(y_first):
                for yy in others_of(y):
                    arrived(e, 2 * yy + c, h)
                    spread(e, yy, h, 0, None)

    def y_stage(k):
        for h in range(y_first, len(ag_spans)):
            for side, ee, cond in side_blocks(k):
                def go(ee=ee, h=h):
                    for yy in others_of(y):
                        arrived(ee, 2 * yy + c, h)
                        sib_copy(ee, yy, h).start()
                guarded(cond, go)

    def hidden_stage(k):
        for side, ee, cond in side_blocks(k):
            def go(ee=ee):
                for h in range(len(ag_spans)):
                    for yy in range(Y):
                        arrived(ee, 2 * yy + (1 - c), h)
                mix[...] = jnp.zeros_like(mix)

                @pl.loop(0, D // ktile)
                def _(i):
                    at = pl.ds(pl.multiple_of(i * ktile, ktile), ktile)
                    mix[...] += jnp.dot(tok[ee, :, at], wgu[at, :], preferred_element_type=F32)
                gate, up = mix[:, :U], mix[:, U:]
                hid[ee] = (gate / (1.0 + jnp.exp(-gate)) * up).astype(BF16)
            guarded(cond, go)

    for k in range(E):
        z_stage(k)
        if k == 1:
            loads[0].wait()
        if k >= 1:
            y_stage(k - 1)
            hidden_stage(k - 1)
    y_stage(E - 1)
    hidden_stage(E - 1)
    loads[1].wait()
    for i, j in others:
        src = cw_all.at[(e + E - i) % E, (yc + EY - j) % EY]
        remote(src, src, cw_s.at[i, j], cw_r.at[(e + E - i) % E, (yc + EY - j) % EY], sib).wait_recv()

    high = (2 * e) // E
    order = []
    for j in range(E):
        a = E - 1 - j // 2 if j % 2 == 0 else j // 2
        order.append(a + high * (E - 1 - 2 * a))

    def own(t, yy, span):
        return part.at[t, rows(2 * yy + c), pl.ds(*span)]

    def rsib_copy(t, yy):
        return remote(part.at[t, rows(2 * yy + 1 - c)], sib_in.at[t, yy], rsib_s.at[t, yy], rsib_r.at[t, yy], sib)

    def ry_copy(i, t, h):
        yy = (y + 1 + i) % Y
        return remote(own(t, yy, rs_spans[h]), y_in.at[i, t, :, pl.ds(*rs_spans[h])], ry_s.at[i, t, h],
                      ry_r.at[i, t, h], {"ey": 2 * yy + c})

    def rz_copy(way, t, h):
        return remote(own(t, y, rs_spans[h]), z_in.at[way, t, :, pl.ds(*rs_spans[h])], rz_s.at[way, t, h],
                      rz_r.at[way, t, h], {"ex": e + 1 - 2 * way})

    pick = (lax.broadcasted_iota(jnp.int32, (R, LANES), 0) == lax.broadcasted_iota(jnp.int32, (R, LANES), 1))

    def local_stage(t):
        cols = [jnp.sum(jnp.where(pick, cw_all[t, cc, pl.ds(yc, 1), :], 0.0), axis=1, keepdims=True) for cc in range(EY)]
        scale = jnp.concatenate(cols, axis=0)

        @pl.loop(0, D // ntile)
        def _(i):
            at = pl.ds(pl.multiple_of(i * ntile, ntile), ntile)
            part[t, :, at] = (jnp.dot(hid[t], wd[:, at], preferred_element_type=F32) * scale).astype(BF16)
        for i in range(Y):
            rsib_copy(t, (y + 1 + i) % Y).start()

    def pair_stage(t):
        for i in range(Y - 1):
            yy = (y + 1 + i) % Y
            rsib_copy(t, yy).wait_recv()
            for h, (lo, n) in enumerate(rs_spans):
                cut = pl.ds(lo, n)
                total = part[t, rows(2 * yy + c), cut].astype(F32) + sib_in[t, yy, :, cut].astype(F32)
                part[t, rows(2 * yy + c), cut] = total.astype(BF16)
                ry_copy(i, t, h).start()

    def line_stage(t):
        rsib_copy(t, y).wait_recv()
        for h, (lo, n) in enumerate(rs_spans):
            cut = pl.ds(lo, n)
            for i in range(Y - 1):
                ry_copy(i, t, h).wait_recv()
            total = part[t, rows(yc), cut].astype(F32) + sib_in[t, y, :, cut].astype(F32)
            for i in range(Y - 1):
                total = total + y_in[i, t, :, cut].astype(F32)
            acc[:, pl.ds(0, n)] = total
            for way, onward, behind in ((0, t > e, e > 0), (1, t < e, e < E - 1)):
                @pl.when(onward & behind)
                def _():
                    rz_copy(way, t, h).wait_recv()
                    acc[:, pl.ds(0, n)] += z_in[way, t, :, cut].astype(F32)
            part[t, rows(yc), cut] = acc[:, pl.ds(0, n)].astype(BF16)
            for way, onward in ((0, t > e), (1, t < e)):
                @pl.when(onward)
                def _():
                    rz_copy(way, t, h).start()

    for j in range(E):
        local_stage(order[j])
        pair_stage(order[j])
        if j >= 1:
            line_stage(order[j - 1])
    line_stage(order[E - 1])
    for h, (lo, n) in enumerate(rs_spans):
        cut = pl.ds(lo, n)
        acc[:, pl.ds(0, n)] = part[e, rows(yc), cut].astype(F32) + tok[e, rows(yc), cut].astype(F32)
        for way, behind in ((0, e > 0), (1, e < E - 1)):
            @pl.when(behind)
            def _():
                rz_copy(way, e, h).wait_recv()
                acc[:, pl.ds(0, n)] += z_in[way, e, :, cut].astype(F32)
        out_ref[:, cut] = acc[:, pl.ds(0, n)].astype(BF16)

    for h in range(len(ag_spans)):
        shift_copy(h).wait_send()
    for i, j in others:
        cw_copy(i, j).wait_send()
    for ee in range(E):
        for h in range(len(ag_spans)):
            for yy in range(Y):
                sib_copy(ee, yy, h).wait_send()
            for i in range(Y - 1):
                if h >= y_first:
                    y_copy(i, ee, h).wait_send()
                else:
                    pl.when(e == ee)(lambda i=i, ee=ee, h=h: y_copy(i, ee, h).wait_send())
            for way, going in ((0, (e >= ee) & (e < E - 1)), (1, (e <= ee) & (e > 0))):
                @pl.when(going)
                def _():
                    for yy in ([y] + others_of(y) if h < y_first else [y]):
                        z_copy(way, ee, yy, h).wait_send()
    for t in range(E):
        for yy in range(Y):
            rsib_copy(t, yy).wait_send()
        for h in range(len(rs_spans)):
            for i in range(Y - 1):
                ry_copy(i, t, h).wait_send()
            for way, going in ((0, t > e), (1, t < e)):
                @pl.when(going)
                def _():
                    rz_copy(way, t, h).wait_send()


def fused(section_out, weights, gate_up, down_rows):
    S, E, EY = lax.axis_size("section"), lax.axis_size("ex"), lax.axis_size("ey")
    Y = EY // 2
    R, D = section_out.shape
    U = down_rows.shape[0]
    ag_spans, y_first = spans_of(D, 4), 1
    rs_spans = even_spans(D, 4)
    na, nr = len(ag_spans), len(rs_spans)
    widest = max(n for _, n in rs_spans)
    dma = pltpu.SemaphoreType.DMA
    kernel = functools.partial(fused_kernel, S, E, EY, R, D, U, weights.shape[0], ag_spans, y_first, rs_spans, 512, 512)
    anywhere, vmem = pl.BlockSpec(memory_space=pl.ANY), pl.BlockSpec(memory_space=pltpu.VMEM)
    return pl.pallas_call(
        kernel,
        out_shape=jax.ShapeDtypeStruct((R, D), BF16),
        in_specs=[anywhere, vmem, anywhere, anywhere],
        out_specs=vmem,
        scratch_shapes=[
            pltpu.VMEM((E, EY * R, D), BF16),
            pltpu.VMEM((E, EY * R, D), BF16),
            pltpu.VMEM((D, 2 * U), BF16),
            pltpu.VMEM((U, D), BF16),
            pltpu.VMEM((E, EY * R, U), BF16),
            pltpu.VMEM((EY * R, 2 * U), F32),
            pltpu.VMEM((R, widest), F32),
            pltpu.VMEM((E, EY) + weights.shape, F32),
            pltpu.VMEM((E, Y, R, D), BF16),
            pltpu.VMEM((Y - 1, E, R, D), BF16),
            pltpu.VMEM((2, E, R, D), BF16),
            dma((2,)), dma((na,)), dma((E, EY, na)), dma((2, E, Y, na)), dma((Y - 1, E, na)), dma((E, Y, na)),
            dma((E, EY)), dma((E, EY)),
            dma((E, Y)), dma((E, Y)), dma((Y - 1, E, nr)), dma((Y - 1, E, nr)), dma((2, E, nr)), dma((2, E, nr)),
        ],
        compiler_params=pltpu.CompilerParams(collective_id=0, has_side_effects=True, vmem_limit_bytes=VMEM_BYTES),
    )(section_out, weights, gate_up, down_rows)


def plain(section_out, own_weights, gate_up, down_rows):
    S = lax.axis_size("section")
    U = down_rows.shape[0]
    incoming = lax.ppermute(section_out, "section", [(i, (i + 1) % S) for i in range(S)])
    tokens = lax.all_gather(incoming, ("ex", "ey"), axis=0, tiled=True)
    scale = lax.all_gather(own_weights, ("ex", "ey"), axis=1, tiled=True)
    scale = lax.dynamic_index_in_dim(scale, lax.axis_index("ey"), 0, keepdims=False)
    mixed = jnp.dot(tokens, gate_up, preferred_element_type=F32)
    hidden = (jax.nn.silu(mixed[:, :U]) * mixed[:, U:]).astype(BF16)
    parts = (jnp.dot(hidden, down_rows, preferred_element_type=F32) * scale[:, None]).astype(BF16)
    total = lax.psum_scatter(parts, ("ex", "ey"), scatter_dimension=0, tiled=True)
    return (incoming.astype(F32) + total.astype(F32)).astype(BF16)


def on_device(section_out, expert_ids, gate_weights, w_gate_up, w_down):
    E, EY = lax.axis_size("ex"), lax.axis_size("ey")
    Y = EY // 2
    R, D = section_out.shape[1:]
    U = w_down.shape[2]
    gate_up = w_gate_up[0, 0].reshape(D, 2 * U)
    down_rows = w_down[0, 0]
    named = expert_ids[0][None] == jnp.arange(EY, dtype=jnp.int32)[:, None, None]
    own_weights = jnp.sum(jnp.where(named, gate_weights[0][None], 0.0), axis=2)
    blocks = 2 * E * EY + E * Y + E * (Y - 1) + 2 * E + 2
    needed = 2 * R * D * blocks + 6 * U * D + EY * R * U * (2 * E + 16) + (1 << 21)
    if needed > VMEM_BYTES or R > LANES:
        return plain(section_out[0], own_weights, gate_up, down_rows)[None]
    padded = jnp.pad(own_weights, ((0, -EY % 8), (0, LANES - R)))
    return fused(section_out[0], padded, gate_up, down_rows)[None]


def solution(mesh):
    return jax.shard_map(
        on_device,
        mesh=mesh,
        in_specs=(
            P("section", ("ex", "ey"), None),
            P("section", ("ex", "ey"), None),
            P("section", ("ex", "ey"), None),
            P("section", "ey", None, None, "ex"),
            P("section", "ey", "ex", None),
        ),
        out_specs=P("section", ("ex", "ey"), None),
        check_vma=False,
    )
```

time: 523 us -> 207 us (0.40)
  waiting for transfers between devices: 419 us -> 0 us
  Pallas kernels: 0 us -> 196 us
  blocking collectives: 36 us -> 0 us
  matrix products: 20.2 us -> 0 us
  between operations: 13.5 us -> 0.01 us
  local copies, waits for them, and re-layouts: 21.7 us -> 10.1 us
  starting transfers between devices: 7.89 us -> 0 us
    pallas_call x0 -> x1, Pallas kernels: none -> 196 us  [fused(): pl.pallas_call(kernel, out_shape=jax.ShapeDtypeStruct((R, D), BF16), in_s...]
    all_gather x1 -> x0, waiting for transfers between devices: 186 us -> none  [on_device(): lax.all_gather(arrived, 'ex', axis=0, tiled=True)]
    reduce_scatter x1 -> x0, waiting for transfers between devices: 185 us -> none  [on_device(): lax.psum_scatter(jnp.dot(hidden_all, down_rows, preferred_element_type=jn...]
    all_to_all x1 -> x0, blocking collectives: 36 us -> none  [on_device(): lax.all_to_all(outgoing.reshape(experts, capacity, model_width), 'ey', sp...]
    all_to_all x1 -> x0, waiting for transfers between devices: 32.4 us -> none  [on_device(): lax.all_to_all(summed.reshape(experts, capacity, model_width), 'ey', spli...]
    dot_general x3 -> x0, matrix products: 20.2 us -> none  [the longest x1 10.9 us: expert_hidden(): mixed = jnp.dot(token_rows, gate_up, preferred_element_type=jnp.float32)]
    ppermute x1 -> x0, waiting for transfers between devices: 16.2 us -> none  [shifted(): return lax.ppermute(value, axis, pairs)]
    gather x2 -> x0, local copies, waits for them, and re-layouts: 9.35 us -> none  [the longest x1 5.5 us: on_device(): picked = expert_out[position].reshape(tok_rows, top_count, model_width)]
  transfers between devices with their start and end apart: 4 -> 0, of which waited for: 4 -> 0; matrix products, arithmetic and copies ran while one was open for 2% -> 0% of each run, Pallas kernels for 0% -> 0%
where the time goes in v1:
time: 207 us
  Pallas kernels  196 us (95%)
  local copies, waits for them, and re-layouts  10.1 us (5%)
    pallas_call x1, Pallas kernels, fused(): pl.pallas_call(kernel, out_shape=jax.ShapeDtypeStruct((R, D), BF16), in_s...  196 us
    unnamed x2, local copies, waits for them, and re-layouts  9.5 us

profile of v1, /device:TPU:0, one launch (start us, length us, event | category | flops | bytes accessed | tf_op | source)
XLA Modules:
  0.0 207.0 jit_solution(6354293439971474299)
XLA Ops:
  0.0 0.7 select_reduce_fusion
  0.7 0.6 pad.4.cw_ref
  1.3 7.3 %copy.8 = bf16[896,8,2,256]{3,1,2,0:T(8,128)(2,1)} copy(bf16[896,8,2,256]{3,2,1,0:T(2,128)(2,1)} %bitcast.9) | data formatting | bytes 14680064
  8.6 196.2 %shard_map.55 = bf16[64,7168]{1,0:T(8,128)(2,1)} custom-call(bf16[64,7168]{1,0:T(8,128)(2,1)} %bitcast.12, f32[8,128]{1,0:T(8,128)} %pad.4.cw_ref, bf16[7168,512]{1,0:T(8,128)(2,1)} %bitcast.8, bf16[256,7168]{1,0:T(8,128)(2,1)} %bitcast.11), custom_call_target="tpu_custom_call" | custom-call | tf_op jit(solution)/shard_map/pallas_call | solution.py:301
  204.9 2.2 %copy.10 = bf16[1,64,7168]{2,1,0:T(8,128)(2,1)} copy(bf16[1,64,7168]{2,1,0:T(8,128)(2,1)} %bitcast.10) | data formatting | bytes 1835008

commit v2 on v1

--- a/solution.py
+++ b/solution.py
@@ -9,6 +9,8 @@
 LANES = 128
 VMEM_BYTES = 67043328
 MESH = pl.DeviceIdType.MESH
+SHIFT_AHEAD = 2
+LAG = 2
 F32, BF16 = jnp.float32, jnp.bfloat16
 
 
@@ -79,7 +81,7 @@
         b = block(ee, cc, h)
         remote(b, b, ss.at[0, 0, 0], ag_r.at[ee, cc, h], sib).wait_recv()
 
-    for h in range(len(ag_spans)):
+    for h in range(SHIFT_AHEAD):
         shift_copy(h).start()
 
     def cw_copy(i, j):
@@ -121,20 +123,20 @@
                 def go(side=side, ee=ee, h=h):
                     first = h < y_first
                     arrived(ee, yc, h)
+                    if k == 0 and h + SHIFT_AHEAD < len(ag_spans):
+                        shift_copy(h + SHIFT_AHEAD).start()
                     if not first or k == 0:
                         for i in range(Y - 1):
                             y_copy(i, ee, h).start()
                     spread(ee, y, h, k, side)
-                    if first and k > 0:
-                        for yy in others_of(y):
-                            arrived(ee, 2 * yy + c, h)
-                            spread(ee, yy, h, k, side)
                 guarded(cond, go)
-        if k == 0:
-            for h in range(y_first):
-                for yy in others_of(y):
-                    arrived(e, 2 * yy + c, h)
-                    spread(e, yy, h, 0, None)
+        for h in range(y_first):
+            for side, ee, cond in side_blocks(k):
+                def go(side=side, ee=ee, h=h):
+                    for yy in others_of(y):
+                        arrived(ee, 2 * yy + c, h)
+                        spread(ee, yy, h, k, side)
+                guarded(cond, go)
 
     def y_stage(k):
         for h in range(y_first, len(ag_spans)):
@@ -209,43 +211,47 @@
         for i in range(Y):
             rsib_copy(t, (y + 1 + i) % Y).start()
 
-    def pair_stage(t):
+    def pair_stage(t, h):
+        cut = pl.ds(*rs_spans[h])
         for i in range(Y - 1):
             yy = (y + 1 + i) % Y
-            rsib_copy(t, yy).wait_recv()
-            for h, (lo, n) in enumerate(rs_spans):
-                cut = pl.ds(lo, n)
-                total = part[t, rows(2 * yy + c), cut].astype(F32) + sib_in[t, yy, :, cut].astype(F32)
-                part[t, rows(2 * yy + c), cut] = total.astype(BF16)
-                ry_copy(i, t, h).start()
-
-    def line_stage(t):
-        rsib_copy(t, y).wait_recv()
-        for h, (lo, n) in enumerate(rs_spans):
-            cut = pl.ds(lo, n)
-            for i in range(Y - 1):
-                ry_copy(i, t, h).wait_recv()
-            total = part[t, rows(yc), cut].astype(F32) + sib_in[t, y, :, cut].astype(F32)
-            for i in range(Y - 1):
-                total = total + y_in[i, t, :, cut].astype(F32)
-            acc[:, pl.ds(0, n)] = total
-            for way, onward, behind in ((0, t > e, e > 0), (1, t < e, e < E - 1)):
-                @pl.when(onward & behind)
-                def _():
-                    rz_copy(way, t, h).wait_recv()
-                    acc[:, pl.ds(0, n)] += z_in[way, t, :, cut].astype(F32)
-            part[t, rows(yc), cut] = acc[:, pl.ds(0, n)].astype(BF16)
-            for way, onward in ((0, t > e), (1, t < e)):
-                @pl.when(onward)
-                def _():
-                    rz_copy(way, t, h).start()
-
-    for j in range(E):
-        local_stage(order[j])
-        pair_stage(order[j])
-        if j >= 1:
-            line_stage(order[j - 1])
-    line_stage(order[E - 1])
+            if h == 0:
+                rsib_copy(t, yy).wait_recv()
+            total = part[t, rows(2 * yy + c), cut].astype(F32) + sib_in[t, yy, :, cut].astype(F32)
+            part[t, rows(2 * yy + c), cut] = total.astype(BF16)
+            ry_copy(i, t, h).start()
+
+    def line_stage(t, h):
+        lo, n = rs_spans[h]
+        cut = pl.ds(lo, n)
+        if h == 0:
+            rsib_copy(t, y).wait_recv()
+        for i in range(Y - 1):
+            ry_copy(i, t, h).wait_recv()
+        total = part[t, rows(yc), cut].astype(F32) + sib_in[t, y, :, cut].astype(F32)
+        for i in range(Y - 1):
+            total = total + y_in[i, t, :, cut].astype(F32)
+        acc[:, pl.ds(0, n)] = total
+        for way, onward, behind in ((0, t > e, e > 0), (1, t < e, e < E - 1)):
+            @pl.when(onward & behind)
+            def _():
+                rz_copy(way, t, h).wait_recv()
+                acc[:, pl.ds(0, n)] += z_in[way, t, :, cut].astype(F32)
+        part[t, rows(yc), cut] = acc[:, pl.ds(0, n)].astype(BF16)
+        for way, onward in ((0, t > e), (1, t < e)):
+            @pl.when(onward)
+            def _():
+                rz_copy(way, t, h).start()
+
+    spans = len(rs_spans)
+    local_stage(order[0])
+    for g in range(E * spans + LAG):
+        if g < E * spans:
+            pair_stage(order[g // spans], g % spans)
+            if g % spans == 1 and g // spans + 1 < E:
+                local_stage(order[g // spans + 1])
+        if g >= LAG:
+            line_stage(order[(g - LAG) // spans], (g - LAG) % spans)
     for h, (lo, n) in enumerate(rs_spans):
         cut = pl.ds(lo, n)
         acc[:, pl.ds(0, n)] = part[e, rows(yc), cut].astype(F32) + tok[e, rows(yc), cut].astype(F32)
@@ -291,8 +297,8 @@
     Y = EY // 2
     R, D = section_out.shape
     U = down_rows.shape[0]
-    ag_spans, y_first = spans_of(D, 4), 1
-    rs_spans = even_spans(D, 4)
+    ag_spans, y_first = spans_of(D, 7), 1
+    rs_spans = even_spans(D, 7)
     na, nr = len(ag_spans), len(rs_spans)
     widest = max(n for _, n in rs_spans)
     dma = pltpu.SemaphoreType.DMA

time: 207 us -> 202 us (0.976)
  Pallas kernels: 196 us -> 191 us
    pallas_call x1, Pallas kernels: 196 us -> 191 us  [fused(): pl.pallas_call(kernel, out_shape=jax.ShapeDtypeStruct((R, D), BF16), in_s...]
where the time goes in v2:
time: 202 us
  Pallas kernels  191 us (95%)
  local copies, waits for them, and re-layouts  10.1 us (5%)
    pallas_call x1, Pallas kernels, fused(): pl.pallas_call(kernel, out_shape=jax.ShapeDtypeStruct((R, D), BF16), in_s...  191 us
    unnamed x2, local copies, waits for them, and re-layouts  9.5 us

profile of v2, /device:TPU:0, one launch (start us, length us, event | category | flops | bytes accessed | tf_op | source)
XLA Modules:
  0.0 202.0 jit_solution(490610112932734575)
XLA Ops:
  0.0 0.7 select_reduce_fusion
  0.7 0.6 pad.4.cw_ref
  1.3 7.3 %copy.8 = bf16[896,8,2,256]{3,1,2,0:T(8,128)(2,1)} copy(bf16[896,8,2,256]{3,2,1,0:T(2,128)(2,1)} %bitcast.9) | data formatting | bytes 14680064
  8.6 191.2 %shard_map.55 = bf16[64,7168]{1,0:T(8,128)(2,1)} custom-call(bf16[64,7168]{1,0:T(8,128)(2,1)} %bitcast.12, f32[8,128]{1,0:T(8,128)} %pad.4.cw_ref, bf16[7168,512]{1,0:T(8,128)(2,1)} %bitcast.8, bf16[256,7168]{1,0:T(8,128)(2,1)} %bitcast.11), custom_call_target="tpu_custom_call" | custom-call | tf_op jit(solution)/shard_map/pallas_call | solution.py:307
  199.8 2.2 %copy.10 = bf16[1,64,7168]{2,1,0:T(8,128)(2,1)} copy(bf16[1,64,7168]{2,1,0:T(8,128)(2,1)} %bitcast.10) | data formatting | bytes 1835008
